TPU v7x, 256 devices: a whole 4x4x8 slice. The times are simulated.
256 devices in a mesh: lat: 8 (over y, core), lon: 32 (over x, z).
Axes of the slice: x: 4, y: 4, z: 8, core: 2. Of those that a mesh axis runs over, the one named last changes fastest.
Arguments:
- ensemble: bfloat16 [8, 4, 32, 1536, 128], P(None, None, 'lat', 'lon'), may hold values from -5 to 5
- vert_loc: float32 [128, 128], replicated, may hold values from -0.5 to 0.5
- static_vert: float32 [128, 128], replicated, may hold values from -0.5 to 0.5
- inst_vert: float32 [16, 128], replicated, may hold values from -0.5 to 0.5
- inst_err: float32 [16], replicated, may hold values from 0.5 to 2
- obs_dest: int32 [65536, 1], P(('lat', 'lon')), may hold values from 0 to 255; in each aligned block of 256 rows (0 to 255, 256 to 511, ...) at most 2 rows name the same one
- obs_patch: int32 [65536], P(('lat', 'lon')), may hold values from 0 to 47
- obs_window: int32 [65536], P(('lat', 'lon')), may hold values from 0 to 3
- obs_inst: int32 [65536], P(('lat', 'lon')), may hold values from 0 to 15
- obs_hweight: float32 [4, 65536], P(None, ('lat', 'lon')), may hold values from 0 to 0.5
- innovation: float32 [65536], P(('lat', 'lon')), may hold values from -6 to 6
- obs_count: int32 [256], P(('lat', 'lon')), may hold values from 128 to 256, as said below
Outputs:
- static_control: float32 [32, 1536, 128], P('lat', 'lon')
- member_control: float32 [8, 32, 1536, 128], P(None, 'lat', 'lon')
- obs_equivalent: float32 [65536], P(('lat', 'lon'))
Inputs may be any that keep to these rules, and one draw needn't show every extreme that they name: `obs_dest`: index of the tile in lat+lon order (lat slowest) that holds the row's patch; within the rows of one shard no tile is named more than 2 times. `obs_patch`: patch p of a tile covers its latitude rows 2 (p // 24) and the next, and its longitude columns 2 (p % 24) and the next. `obs_count`: some shard uses all 256 rows in every draw; rows at or past a shard's count are unused.
All inputs are finite; a program needn't handle non-finite values.
Results may differ from a plain program's by a relative error of at most 0.0003.
Values sent between devices are 32-bit elements; how exact they have to be, the bound alone decides.
A program may use at most 64 MiB of HBM per device.

v0:
```python
import jax
import jax.numpy as jnp
from jax import lax
from jax.experimental import pallas as pl
from jax.experimental.pallas import tpu as pltpu
from jax.sharding import PartitionSpec as P

F32 = jnp.float32
HI = lax.Precision.HIGHEST
MESH = pl.DeviceIdType.MESH
SMOOTH = 0.15
BETA_STATIC = 0.5
BETA_ENSEMBLE = 0.85
NLAT, NLON = 8, 32
MEM, WIN, ROWS, COLS, LEV, NINST = 8, 4, 4, 48, 128, 16
FIELDS = MEM + 1
CELLS = ROWS * COLS
OBS = 256
PAD = 8
WIDE = COLS + 2 * PAD
TALL = 3 * ROWS
OWN = pl.ds(PAD, COLS)


def dot(a, b, precision=HI):
    return lax.dot_general(
        a, b, (((1,), (0,)), ((), ())), precision=precision, preferred_element_type=F32
    )


def dot_t(a, b, precision=HI):
    return lax.dot_general(
        a, b, (((1,), (1,)), ((), ())), precision=precision, preferred_element_type=F32
    )


def iota(shape, dim):
    return lax.broadcasted_iota(jnp.int32, shape, dim)


def total(x):
    return jnp.sum(jnp.sum(x, axis=1, keepdims=True), axis=0, keepdims=True)


def kernel(
    ens_hbm, vert_ref, static_ref, inst_ref, err_ref, dest_col_ref, dest_row_ref,
    patch_ref, window_ref, instr_ref, hweight_ref, innov_ref, count_ref,
    out_static, out_member, out_equiv,
    ens, send1, first1, flat1, second1, send2, first2, flat2, second2,
    red_a_send, red_a, red_b_send, red_b,
    place, onehot, onehot_t, spread_w, rinv, obs_e, obs_z, grad, incr,
    reg, strip_send, strip_recv, stage_a, stage_b, resid, acc,
    ens_sem, x1s, x1r, y1s, y1r, x2s, x2r, y2s, y2r, ras, rar, rbs, rbr, hs, hr,
):
    lat = lax.axis_index("lat")
    lon = lax.axis_index("lon")
    has_n = lat > 0
    has_s = lat < NLAT - 1
    west = lax.rem(lon + NLON - 1, NLON)
    east = lax.rem(lon + 1, NLON)
    base = lat * 16

    ens_copy = pltpu.make_async_copy(ens_hbm, ens, ens_sem)
    ens_copy.start()

    barrier = pltpu.get_barrier_semaphore()

    def greet(i, j):
        pl.semaphore_signal(barrier, inc=1, device_id=(i, j), device_id_type=MESH)

    def greet_lon(d, c):
        greet(lat, lax.rem(lon + d, NLON))
        return c

    def greet_lat(d, c):
        greet(lax.rem(lat + d, NLAT), lon)
        return c

    lax.fori_loop(1, NLON, greet_lon, 0)
    lax.fori_loop(1, NLAT, greet_lat, 0)

    for step in (1, NLAT - 1):
        greet(lax.rem(lat + step, NLAT), west)
        greet(lax.rem(lat + step, NLAT), east)

    dest_row = dest_row_ref[...]
    same = (dest_col_ref[...] == dest_row) & (iota((OBS, OBS), 0) < iota((OBS, OBS), 1))
    rank = jnp.sum(same.astype(F32), axis=0, keepdims=True)
    group = (dest_row >> 5) * 2 + rank.astype(jnp.int32)
    active = (iota((1, OBS), 1) < count_ref[...]).astype(F32)
    words = jnp.concatenate(
        [
            patch_ref[...].astype(F32),
            window_ref[...].astype(F32),
            instr_ref[...].astype(F32),
            hweight_ref[...] * active,
            innov_ref[...],
        ],
        axis=0,
    )
    tiled = jnp.concatenate([words] * 16, axis=0)
    tiled = jnp.where((iota((128, OBS), 0) >> 3) == group, tiled, 0.0)
    to_lon = (iota((NLON, OBS), 0) == (dest_row & 31)).astype(F32)
    outgoing = dot_t(to_lon, tiled)
    for j in range(NLON):
        send1[j] = outgoing[j : j + 1, :]

    place[...] = jnp.zeros_like(place)
    for c in range(4):
        place[c, 16 * c : 16 * c + 16, :] = inst_ref[...]
    for a in range(2):
        reg[a, :, :, 0:PAD, :] = jnp.zeros((FIELDS, TALL, PAD, LEV), F32)
        reg[a, :, :, PAD + COLS : WIDE, :] = jnp.zeros((FIELDS, TALL, PAD, LEV), F32)
    acc[...] = jnp.zeros_like(acc)

    pl.semaphore_wait(barrier, NLON - 1 + NLAT - 1 + 4)

    def remote(src, dst, ssem, rsem, i, j):
        return pltpu.make_async_remote_copy(
            src_ref=src, dst_ref=dst, send_sem=ssem, recv_sem=rsem,
            device_id=(i, j), device_id_type=MESH,
        )

    def rows_to_lon(send, first, ssem, rsem, one_row):
        def go(d, c):
            j = lax.rem(lon + d, NLON)
            src = send if one_row else send.at[j]
            remote(src, first.at[lon], ssem.at[j], rsem.at[lon], lat, j).start()
            return c

        lax.fori_loop(1, NLON, go, 0)
        first[lon] = send[...] if one_row else send[lon]

    def end_lon(send, first, ssem, rsem, one_row):
        def done(d, c):
            j = lax.rem(lon + d, NLON)
            src = send if one_row else send.at[j]
            remote(src, first.at[j], ssem.at[j], rsem.at[j], lat, j).wait()
            return c

        lax.fori_loop(1, NLON, done, 0)

    def block_to_lat(send, second, ssem, rsem):
        def go(d, c):
            i = lax.rem(lat + d, NLAT)
            remote(send, second.at[lat], ssem.at[i], rsem.at[lat], i, lon).start()
            return c

        lax.fori_loop(1, NLAT, go, 0)
        second[lat] = send[...]

    def end_lat(send, second, ssem, rsem):
        def done(d, c):
            i = lax.rem(lat + d, NLAT)
            remote(send, second.at[i], ssem.at[i], rsem.at[i], i, lon).wait()
            return c

        lax.fori_loop(1, NLAT, done, 0)

    def exchange(send, first, flat, second, xs, xr, ys, yr):
        rows_to_lon(send, first, xs, xr, False)
        end_lon(send, first, xs, xr, False)
        for j in range(NLON):
            flat[j : j + 1, :] = first[j]
        block_to_lat(flat, second, ys, yr)
        end_lat(flat, second, ys, yr)
        return second[...].reshape(NLAT * NLON, 128)

    received = exchange(send1, first1, flat1, second1, x1s, x1r, y1s, y1r)

    lane = iota((OBS, 128), 1)
    inst_lane = (lane & 15).astype(F32)
    err_row = err_ref[...]
    rinv_row = 1.0 / (err_row * err_row)
    row_w = iota((128, 128), 0)
    col_w = iota((128, 128), 1)
    for s in range(2):
        at = base + 8 * s
        l0 = iota((128, OBS), 0)
        pick = jnp.where(l0 == at, 1.0, 0.0) + jnp.where(l0 == at + 1, 48.0, 0.0)
        l1 = iota((OBS, 128), 1)
        pick_t = jnp.where(l1 == at, 1.0, 0.0) + jnp.where(l1 == at + 1, 48.0, 0.0)
        onehot[s] = (dot(received, pick) == iota((OBS, OBS), 1).astype(F32)).astype(F32)
        onehot_t[s] = (
            dot_t(pick_t, received) == iota((OBS, OBS), 0).astype(F32)
        ).astype(F32)
        instr = dot(received, jnp.where(row_w == at + 2, 1.0, 0.0))
        corner = jnp.where((row_w == at + 3 + (col_w >> 4)) & (col_w < 64), 1.0, 0.0)
        hit = instr == inst_lane
        spread_w[s] = jnp.where(hit, dot(received, corner), 0.0)
        err_hit = jnp.where(hit & (lane < 16), rinv_row, 0.0)
        inv = jnp.sum(err_hit, axis=1, keepdims=True)
        rinv[s] = jnp.broadcast_to(inv, (OBS, 128))
        obs_z[s] = dot(received, jnp.where(row_w == at + 7, 1.0, 0.0))

    ens_copy.wait()

    def gradient(weights):
        table = dot(onehot_t[0], spread_w[0] * (rinv[0] * weights[0])) + dot(
            onehot_t[1], spread_w[1] * (rinv[1] * weights[1])
        )
        table = table[:CELLS]
        for c in range(4):
            field = dot(table, place[c])
            for t in range(WIN):
                for pr in range(2):
                    at = (t * 2 + pr) * 24
                    grad[t, 2 * pr + c // 2, pl.ds(c % 2, 24, stride=2), :] = field[
                        at : at + 24
                    ]

    def halo_copies(a, k):
        own = reg.at[a, k, pl.ds(ROWS, ROWS), OWN]
        north_rows = reg.at[a, k, pl.ds(0, ROWS), OWN]
        south_rows = reg.at[a, k, pl.ds(2 * ROWS, ROWS), OWN]
        w_strip = strip_send.at[a, k, 0]
        e_strip = strip_send.at[a, k, 1]

        def one(src, dst, slot, i, j):
            return remote(src, dst, hs.at[a, slot, k], hr.at[a, slot, k], i, j)

        always = [
            one(w_strip, strip_recv.at[a, k, 1, 1], 3, lat, west),
            one(e_strip, strip_recv.at[a, k, 0, 1], 2, lat, east),
        ]
        if_n = [
            one(own, south_rows, 1, lat - 1, lon),
            one(w_strip, strip_recv.at[a, k, 1, 2], 7, lat - 1, west),
            one(e_strip, strip_recv.at[a, k, 0, 2], 6, lat - 1, east),
        ]
        if_s = [
            one(own, north_rows, 0, lat + 1, lon),
            one(w_strip, strip_recv.at[a, k, 1, 0], 5, lat + 1, west),
            one(e_strip, strip_recv.at[a, k, 0, 0], 4, lat + 1, east),
        ]
        return always, if_n, if_s

    def start_halo(a, k):
        always, if_n, if_s = halo_copies(a, k)

        @pl.when(has_n)
        def _():
            for c in if_n:
                c.start()

        @pl.when(has_s)
        def _():
            for c in if_s:
                c.start()

        for c in always:
            c.start()

    def wait_halo(a, k):
        always, if_n, if_s = halo_copies(a, k)
        for c in always:
            c.wait_recv()

        @pl.when(has_n)
        def _():
            for c in if_s:
                c.wait_recv()

        @pl.when(has_s)
        def _():
            for c in if_n:
                c.wait_recv()

    def wait_sent(a, k):
        always, if_n, if_s = halo_copies(a, k)
        for c in always:
            c.wait_send()

        @pl.when(has_n)
        def _():
            for c in if_n:
                c.wait_send()

        @pl.when(has_s)
        def _():
            for c in if_s:
                c.wait_send()

    def put_own(a, k, flat):
        for r in range(ROWS):
            row = flat[r * COLS : (r + 1) * COLS]
            reg[a, k, ROWS + r, PAD : PAD + COLS, :] = row
            strip_send[a, k, 0, 4 * r : 4 * r + 4, :] = row[0:4]
            strip_send[a, k, 1, 4 * r : 4 * r + 4, :] = row[COLS - 4 : COLS]

    def send_fields(a):
        def member(k, c):
            summed = ens[k, 0].astype(F32) * grad[0]
            for t in range(1, WIN):
                summed = summed + ens[k, t].astype(F32) * grad[t]
            flat = dot_t(summed.reshape(CELLS, LEV), vert_ref[...])
            put_own(a, k, BETA_ENSEMBLE * flat)
            start_halo(a, k)
            return c

        lax.fori_loop(0, MEM, member, 0)
        summed = (grad[0] + grad[1]) + (grad[2] + grad[3])
        flat = dot_t(summed.reshape(CELLS, LEV), static_ref[...])
        put_own(a, MEM, BETA_STATIC * flat)
        start_halo(a, MEM)

    def smooth(up, mid, down):
        side = pltpu.roll(mid, 1, 0) + pltpu.roll(mid, WIDE - 1, 0)
        return (1.0 - 4.0 * SMOOTH) * mid + SMOOTH * (up + down + side)

    def keep(row, value):
        if row < ROWS:
            return jnp.where(has_n, value, 0.0)
        if row >= 2 * ROWS:
            return jnp.where(has_s, value, 0.0)
        return value

    def spread_twice(a, k):
        for side, col in ((0, PAD - 4), (1, PAD + COLS)):
            for part in range(3):
                for r in range(ROWS):
                    reg[a, k, part * ROWS + r, col : col + 4, :] = strip_recv[
                        a, k, side, part, 4 * r : 4 * r + 4, :
                    ]

        def sweep(read, write, low, high):
            rows = [read(low - 1), read(low)]
            for r in range(low, high):
                rows.append(read(r + 1))
                write(r, keep(r, smooth(rows[0], rows[1], rows[2])))
                rows = rows[1:]

        def to_a(r, v):
            stage_a[r] = v

        def to_b(r, v):
            stage_b[r] = v

        sweep(lambda r: keep(r, reg[a, k, r]), to_a, 1, TALL - 1)
        sweep(lambda r: stage_a[r], to_b, 2, TALL - 2)
        for r in range(ROWS):
            resid[a, k, r] = stage_b[ROWS + r, PAD : PAD + COLS, :]
        sweep(lambda r: stage_b[r], to_a, 3, TALL - 3)
        sweep(lambda r: stage_a[r], to_b, 4, TALL - 4)
        rows = [stage_b[ROWS + r, PAD : PAD + COLS, :] for r in range(ROWS)]
        return jnp.concatenate(rows, axis=0)

    def apply_fields(a, target):
        wait_halo(a, MEM)
        part = BETA_STATIC * dot(spread_twice(a, MEM), static_ref[...])
        part = part.reshape(ROWS, COLS, LEV)
        for t in range(WIN):
            incr[t] = part

        def member(k, c):
            wait_halo(a, k)
            local = BETA_ENSEMBLE * dot(spread_twice(a, k), vert_ref[...])
            local = local.reshape(ROWS, COLS, LEV)
            for t in range(WIN):
                incr[t] += ens[k, t].astype(F32) * local
            return c

        lax.fori_loop(0, MEM, member, 0)
        seen = jnp.zeros((CELLS, 128), F32)
        for c in range(4):
            cells = [
                incr[t, 2 * pr + c // 2, pl.ds(c % 2, 24, stride=2), :]
                for t in range(WIN)
                for pr in range(2)
            ]
            seen = seen + dot_t(jnp.concatenate(cells, axis=0), place[c])
        seen = jnp.concatenate([seen, jnp.zeros((OBS - CELLS, 128), F32)], axis=0)
        for s in range(2):
            value = dot(onehot[s], seen) * spread_w[s]
            value = jnp.sum(value, axis=1, keepdims=True)
            target[s] = jnp.broadcast_to(value, (OBS, 128))

    gradient(obs_z)
    send_fields(0)
    apply_fields(0, obs_e)

    def square(k, c):
        for r in range(ROWS):
            v = resid[0, k, r]
            acc[0] += jnp.sum((v * v).reshape(COLS // 8, 8, LEV), axis=0)
        return c

    lax.fori_loop(0, FIELDS, square, 0)
    sum_a = total(acc[0])
    sum_b = jnp.zeros((1, 1), F32)
    for s in range(2):
        e = obs_e[s]
        sum_b = sum_b + jnp.sum(rinv[s] * e * e, axis=0, keepdims=True)[:, 0:1]
    lane1 = iota((1, 128), 1)
    red_a_send[...] = jnp.where(lane1 == 0, sum_a, 0.0) + jnp.where(lane1 == 1, sum_b, 0.0)

    block_to_lat(red_a_send, red_a, ras, rar)
    gradient(obs_e)
    send_fields(1)
    end_lat(red_a_send, red_a, ras, rar)
    part = red_a[0]
    for i in range(1, NLAT):
        part = part + red_a[i]
    red_b_send[...] = part
    rows_to_lon(red_b_send, red_b, rbs, rbr, True)
    apply_fields(1, obs_z)
    end_lon(red_b_send, red_b, rbs, rbr, True)
    whole = red_b[0]
    for j in range(1, NLON):
        whole = whole + red_b[j]
    a0 = whole[:, 0:1]
    b0 = whole[:, 1:2]
    step0 = a0 / (a0 + b0)

    acc[...] = jnp.zeros_like(acc)

    def next_residual(k, c):
        for r in range(ROWS):
            r0 = resid[0, k, r]
            r1 = (1.0 - step0) * r0 - step0 * resid[1, k, r]
            resid[1, k, r] = r1
            acc[0] += jnp.sum((r1 * r1).reshape(COLS // 8, 8, LEV), axis=0)
            acc[1] += jnp.sum((r1 * r0).reshape(COLS // 8, 8, LEV), axis=0)
        return c

    lax.fori_loop(0, FIELDS, next_residual, 0)
    partial = [total(acc[0]), total(acc[1])]
    sum_v = jnp.zeros((1, 1), F32)
    sum_w = jnp.zeros((1, 1), F32)
    blocks = jnp.zeros((OBS, 128), F32)
    word = lane & 15
    for s in range(2):
        e = obs_e[s]
        nxt = (1.0 - step0) * e - step0 * obs_z[s]
        sum_v = sum_v + jnp.sum(rinv[s] * nxt * nxt, axis=0, keepdims=True)[:, 0:1]
        sum_w = sum_w + jnp.sum(rinv[s] * nxt * e, axis=0, keepdims=True)[:, 0:1]
        blocks = jnp.where(word == s, e, blocks)
        blocks = jnp.where(word == 2 + s, nxt, blocks)
    partial = partial + [sum_v, sum_w]
    for n in range(4):
        blocks = jnp.where(word == 4 + n, partial[n], blocks)
    blocks = jnp.where((lane >> 4) == (iota((OBS, 128), 0) >> 5), blocks, 0.0)
    out_rows = blocks[0:NLON]
    for i in range(1, NLAT):
        out_rows = out_rows + blocks[i * NLON : (i + 1) * NLON]
    for j in range(NLON):
        send2[j] = out_rows[j : j + 1, :]

    back = exchange(send2, first2, flat2, second2, x2s, x2r, y2s, y2r)
    sums = jnp.sum(back, axis=0, keepdims=True)
    got = [
        jnp.sum(jnp.where(lane1 == base + 4 + n, sums, 0.0), axis=1, keepdims=True)
        for n in range(4)
    ]
    rr1, u, v, w = got
    ratio = rr1 / a0
    below = (rr1 + 2.0 * ratio * u + ratio * ratio * a0) + (
        v + 2.0 * ratio * w + ratio * ratio * b0
    )
    step1 = rr1 / below
    c0 = step0 + step1 * ratio
    c1 = step1

    def finish(k, c):
        for r in range(ROWS):
            out_member[k, r] = c0 * resid[0, k, r] + c1 * resid[1, k, r]
        return c

    lax.fori_loop(0, MEM, finish, 0)
    for r in range(ROWS):
        out_static[r] = c0 * resid[0, MEM, r] + c1 * resid[1, MEM, r]

    mine = dest_row == iota((OBS, OBS), 0)
    equiv = jnp.zeros((1, OBS), F32)
    for s in range(2):
        mix = jnp.where(lane1 == base + s, c0, 0.0) + jnp.where(lane1 == base + 2 + s, c1, 0.0)
        value = jnp.sum(back * mix, axis=1, keepdims=True)
        chosen = jnp.where(mine & (rank == float(s)), value, 0.0)
        equiv = equiv + jnp.sum(chosen, axis=0, keepdims=True)
    out_equiv[...] = equiv

    def drain(k, c):
        wait_sent(0, k)
        wait_sent(1, k)
        return c

    lax.fori_loop(0, FIELDS, drain, 0)


def body(
    ensemble, vert_loc, static_vert, inst_vert, inst_err, obs_dest, obs_patch,
    obs_window, obs_inst, obs_hweight, innovation, obs_count,
):
    vmem = pl.BlockSpec(memory_space=pltpu.VMEM)
    dma = pltpu.SemaphoreType.DMA
    scratch = [
        pltpu.VMEM((MEM, WIN, ROWS, COLS, LEV), jnp.bfloat16),
        pltpu.VMEM((NLON, 1, 128), F32),
        pltpu.VMEM((NLON, 1, 128), F32),
        pltpu.VMEM((NLON, 128), F32),
        pltpu.VMEM((NLAT, NLON, 128), F32),
        pltpu.VMEM((NLON, 1, 128), F32),
        pltpu.VMEM((NLON, 1, 128), F32),
        pltpu.VMEM((NLON, 128), F32),
        pltpu.VMEM((NLAT, NLON, 128), F32),
        pltpu.VMEM((1, 128), F32),
        pltpu.VMEM((NLAT, 1, 128), F32),
        pltpu.VMEM((1, 128), F32),
        pltpu.VMEM((NLON, 1, 128), F32),
        pltpu.VMEM((4, 128, LEV), F32),
        pltpu.VMEM((2, OBS, OBS), F32),
        pltpu.VMEM((2, OBS, OBS), F32),
        pltpu.VMEM((2, OBS, 128), F32),
        pltpu.VMEM((2, OBS, 128), F32),
        pltpu.VMEM((2, OBS, 128), F32),
        pltpu.VMEM((2, OBS, 128), F32),
        pltpu.VMEM((WIN, ROWS, COLS, LEV), F32),
        pltpu.VMEM((WIN, ROWS, COLS, LEV), F32),
        pltpu.VMEM((2, FIELDS, TALL, WIDE, LEV), F32),
        pltpu.VMEM((2, FIELDS, 2, 16, LEV), F32),
        pltpu.VMEM((2, FIELDS, 2, 3, 16, LEV), F32),
        pltpu.VMEM((TALL, WIDE, LEV), F32),
        pltpu.VMEM((TALL, WIDE, LEV), F32),
        pltpu.VMEM((2, FIELDS, ROWS, COLS, LEV), F32),
        pltpu.VMEM((2, 8, LEV), F32),
        dma(()),
        dma((NLON,)), dma((NLON,)), dma((NLAT,)), dma((NLAT,)),
        dma((NLON,)), dma((NLON,)), dma((NLAT,)), dma((NLAT,)),
        dma((NLAT,)), dma((NLAT,)), dma((NLON,)), dma((NLON,)),
        dma((2, 8, FIELDS)), dma((2, 8, FIELDS)),
    ]
    static_out, member_out, equiv = pl.pallas_call(
        kernel,
        out_shape=(
            jax.ShapeDtypeStruct((ROWS, COLS, LEV), F32),
            jax.ShapeDtypeStruct((MEM, ROWS, COLS, LEV), F32),
            jax.ShapeDtypeStruct((1, OBS), F32),
        ),
        in_specs=[pl.BlockSpec(memory_space=pl.ANY)] + [vmem] * 12,
        out_specs=(vmem, vmem, vmem),
        scratch_shapes=scratch,
        compiler_params=pltpu.CompilerParams(
            collective_id=0, has_side_effects=True, vmem_limit_bytes=56 << 20
        ),
        name="inner_loop",
    )(
        ensemble, vert_loc, static_vert, inst_vert,
        jnp.tile(inst_err, 8).reshape(1, 128),
        obs_dest, obs_dest.reshape(1, OBS), obs_patch.reshape(1, OBS),
        obs_window.reshape(1, OBS), obs_inst.reshape(1, OBS), obs_hweight,
        innovation.reshape(1, OBS), obs_count.reshape(1, 1),
    )
    return static_out, member_out, equiv.reshape(OBS)


def solution(mesh):
    both = ("lat", "lon")
    in_specs = (
        P(None, None, "lat", "lon", None), P(), P(), P(), P(), P(both, None),
        P(both), P(both), P(both), P(None, both), P(both), P(both),
    )
    out_specs = (P("lat", "lon", None), P(None, "lat", "lon", None), P(both))
    return jax.shard_map(
        body, mesh=mesh, in_specs=in_specs, out_specs=out_specs, check_vma=False
    )
```

profile of v0, /device:TPU:1, one launch (start us, length us, event | category | flops | bytes accessed | tf_op | source)
XLA Modules:
  0.0 96.0 jit_solution(7442274412743890010)
XLA Ops:
  1.3 0.7 tile.2
  1.9 0.6 reshape_tile.3.err_ref
  2.5 1.5 %copy.15.dest_col_ref = s32[256,1]{1,0:T(8,128)} copy(s32[256,1]{0,1:T(1,128)} %param.17) | data formatting | bytes 2048 | tf_op args[5]
  4.0 87.8 %inner_loop.1 = (f32[4,48,128]{2,1,0:T(8,128)}, f32[8,4,48,128]{3,2,1,0:T(8,128)}, f32[1,256]{1,0:T(1,128)}) custom-call(bf16[8,4,4,48,128]{4,3,2,1,0:T(8,128)(2,1)} %ens_hbm.1, f32[128,128]{1,0:T(8,128)} %vert_ref.1, f32[128,128]{1,0:T(8,128)} %static_ref.1, f32[16,128]{1,0:T(8,128)} %inst_ref.1, f32[1,128]{1,0:T(1,128)} %reshape_tile.3.err_ref, ...), custom_call_target="tpu_custom_call" | custom-call | tf_op jit(solution)/shard_map/inner_loop/pallas_call | solution.py:532
  91.8 0.0 copy-start
  91.8 1.5 %copy.20 = f32[4,48,128]{2,1,0:T(8,128)} copy(f32[4,48,128]{2,1,0:T(8,128)} %get-tuple-element.12) | data formatting | bytes 196608
  93.3 2.1 %copy.21 = f32[8,4,48,128]{3,2,1,0:T(8,128)} copy(f32[8,4,48,128]{3,2,1,0:T(8,128)} %get-tuple-element.13) | data formatting | bytes 1572864
  95.4 0.0 copy-done
  95.4 0.6 copy.22
Async XLA Ops:
  91.8 3.6 %copy-start = (f32[1,256]{1,0:T(1,128)S(1)}, f32[1,256]{1,0:T(1,128)}, u32[]{:S(2)}) copy-start(f32[1,256]{1,0:T(1,128)} %get-tuple-element.8) | copy-start | bytes 3076
where the time goes:
time: 96.2 us; the launch traced here: 96 us
  Pallas kernels  87.8 us (91%)
  local copies, waits for them, and re-layouts  6.9 us (7%)
  between operations  1.3 us (1%)
    pallas_call x1, Pallas kernels, body(): pl.pallas_call(kernel, out_shape=(jax.ShapeDtypeStruct((ROWS, COLS, LEV),...  87.8 us
    unnamed x6, local copies, waits for them, and re-layouts  5.65 us

commit v1 on v0

v1 whole, which is shorter than its diff:
```python
import jax
import jax.numpy as jnp
from jax import lax
from jax.experimental import pallas as pl
from jax.experimental.pallas import tpu as pltpu
from jax.sharding import PartitionSpec as P

F32 = jnp.float32
BF16 = jnp.bfloat16
MESH = pl.DeviceIdType.MESH
SMOOTH = 0.15
BETA_STATIC = 0.5
BETA_ENSEMBLE = 0.85
NLAT, NLON = 8, 32
MEM, WIN, ROWS, COLS, LEV, NINST = 8, 4, 4, 48, 128, 16
FIELDS = MEM + 1
CELLS = ROWS * COLS
OBS = 256
SLOTS = 2 * OBS
PAD = 8
WIDE = COLS + 2 * PAD
TALL = 3 * ROWS
OWN = pl.ds(PAD, COLS)


def dot(a, b, precision=None):
    return lax.dot_general(
        a, b, (((1,), (0,)), ((), ())), precision=precision, preferred_element_type=F32
    )


def dot_t(a, b, precision=None):
    return lax.dot_general(
        a, b, (((1,), (1,)), ((), ())), precision=precision, preferred_element_type=F32
    )


def split(x):
    high = x.astype(BF16)
    return high, (x - high.astype(F32)).astype(BF16)


def dot3(x, w_high, w_low):
    high, low = split(x)
    return dot(high, w_high) + (dot(low, w_high) + dot(high, w_low))


def pick_rows(onehot, x):
    high, low = split(x)
    return dot(onehot, high) + dot(onehot, low)


def iota(shape, dim):
    return lax.broadcasted_iota(jnp.int32, shape, dim)


def total(x):
    return jnp.sum(jnp.sum(x, axis=1, keepdims=True), axis=0, keepdims=True)


def fold(x):
    return jnp.sum(x.reshape(COLS // 8, 8, LEV), axis=0)


def kernel(
    count_ref, ens_hbm, vert_hbm, static_hbm, inst_hbm, err_hbm, dest_hbm,
    patch_hbm, window_hbm, instr_hbm, hweight_hbm, innov_hbm,
    out_fields, out_coef, out_equiv,
    ens, vert_ref, static_ref, inst_ref, err_ref, dest_ref,
    patch_ref, window_ref, instr_ref, hweight_ref, innov_ref,
    err_wide, send1, first1, block1, second1, send2, first2, block2, second2, arrived,
    red_a_send, red_a, red_b_send, red_b,
    level_w, place_f, place_w, place_wt, onehot, onehot_t, spread_w, rinv, obs_e, obs_z,
    grad, incr, reg, strip_send, strip_recv, corner_send, corner_recv, tally, stage_a, stage_b, resid, acc,
    in_sem, ens_sem, out_sem, x1, y1, x2, y2, ra, rb, hs, hr,
):
    lat = lax.axis_index("lat")
    lon = lax.axis_index("lon")
    has_n = lat > 0
    has_s = lat < NLAT - 1
    west = lax.rem(lon + NLON - 1, NLON)
    east = lax.rem(lon + 1, NLON)

    barrier = pltpu.get_barrier_semaphore()

    def greet(i, j):
        pl.semaphore_signal(barrier, inc=1, device_id=(i, j), device_id_type=MESH)

    def greet_lon(d, c):
        greet(lat, lax.rem(lon + d, NLON))
        return c

    def greet_lat(d, c):
        greet(lax.rem(lat + d, NLAT), lon)
        return c

    small = [
        (dest_hbm, dest_ref), (patch_hbm, patch_ref), (window_hbm, window_ref),
        (instr_hbm, instr_ref), (hweight_hbm, hweight_ref), (innov_hbm, innov_ref),
        (vert_hbm, vert_ref), (static_hbm, static_ref), (inst_hbm, inst_ref),
        (err_hbm, err_ref),
    ]
    loads = [
        pltpu.make_async_copy(a, b, in_sem.at[n]) for n, (a, b) in enumerate(small)
    ]
    for c in loads:
        c.start()
    lax.fori_loop(1, NLON, greet_lon, 0)
    lax.fori_loop(1, NLAT, greet_lat, 0)
    for step in (1, NLAT - 1):
        greet(lax.rem(lat + step, NLAT), west)
        greet(lax.rem(lat + step, NLAT), east)
    ens_copy = pltpu.make_async_copy(ens_hbm, ens, ens_sem)
    ens_copy.start()
    for c in loads:
        c.wait()

    dest_row = dest_ref[...]
    square0 = iota((OBS, OBS), 0)
    square1 = iota((OBS, OBS), 1)
    dest_f = jnp.where(square0 == square1, dest_row.astype(F32), 0.0)
    dest_col = jnp.sum(dest_f, axis=1, keepdims=True)
    same = (dest_col == dest_row.astype(F32)) & (square0 < square1)
    rank = jnp.sum(same.astype(F32), axis=0, keepdims=True)
    group = (7 - (dest_row >> 5)) * 2 + rank.astype(jnp.int32)
    active = (iota((1, OBS), 1) < count_ref[0]).astype(F32)
    words = jnp.concatenate(
        [
            patch_ref[...].astype(F32),
            window_ref[...].astype(F32),
            instr_ref[...].astype(F32),
            hweight_ref[...] * active,
            innov_ref[...],
        ],
        axis=0,
    )
    tiled = jnp.concatenate([words] * 16, axis=0)
    tiled = jnp.where((iota((128, OBS), 0) >> 3) == group, tiled, 0.0)
    to_lon = (iota((NLON, OBS), 0) == (dest_row & 31)).astype(F32)
    outgoing = dot_t(to_lon, tiled, lax.Precision.HIGHEST)
    for j in range(NLON):
        send1[j] = outgoing[j : j + 1, :]

    err_wide[...] = jnp.ones_like(err_wide)
    err_wide[:, 0:NINST] = err_ref[...]
    for n, ref in enumerate((vert_ref, static_ref)):
        w = ref[...]
        level_w[n, 0], level_w[n, 1] = split(w)
        level_w[n, 2], level_w[n, 3] = split(w.T)
    place_f[...] = jnp.zeros_like(place_f)
    for c in range(4):
        place_f[16 * c : 16 * c + 16, LEV * c : LEV * c + LEV] = inst_ref[...]
    for n, half in enumerate(split(place_f[...])):
        place_w[n] = half
    for c in range(4):
        for n, half in enumerate(split(place_f[:, LEV * c : LEV * c + LEV].T)):
            place_wt[n, LEV * c : LEV * c + LEV, :] = half
    for a in range(2):
        reg[a, :, :, 0:PAD, :] = jnp.zeros((FIELDS, TALL, PAD, LEV), F32)
        reg[a, :, :, PAD + COLS : WIDE, :] = jnp.zeros((FIELDS, TALL, PAD, LEV), F32)
    acc[...] = jnp.zeros_like(acc)
    incr[...] = jnp.zeros_like(incr)

    pl.semaphore_wait(barrier, NLON - 1 + NLAT - 1 + 4)

    def remote(src, dst, ssem, rsem, i, j):
        return pltpu.make_async_remote_copy(
            src_ref=src, dst_ref=dst, send_sem=ssem, recv_sem=rsem,
            device_id=(i, j), device_id_type=MESH,
        )

    def rows_done(rows, ssem, rsem):
        ref = tally.at[pl.ds(0, rows)]
        return remote(ref, ref, ssem, rsem, lat, east)

    def rows_to_lon(send, first, sems, one_row):
        def go(d, c):
            j = lax.rem(lon + d, NLON)
            src = send if one_row else send.at[j]
            remote(src, first.at[lon], sems.at[0], sems.at[1], lat, j).start()
            return c

        lax.fori_loop(1, NLON, go, 0)
        first[lon] = send[...] if one_row else send[lon]

    def all_lon(sems):
        return rows_done(NLON - 1, sems.at[0], sems.at[1])

    def block_to_lat(send, second, sems, whole):
        def go(d, c):
            i = lax.rem(lat + d, NLAT)
            src = send if whole else send.at[i]
            remote(src, second.at[lat], sems.at[0], sems.at[1], i, lon).start()
            return c

        lax.fori_loop(1, NLAT, go, 0)
        second[lat] = send[...] if whole else send[lat]

    def all_lat(sems, rows):
        return rows_done((NLAT - 1) * rows, sems.at[0], sems.at[1])

    lanes8 = iota((8, 128), 1) >> 4

    def exchange(send, first, block, second, xs, ys):
        rows_to_lon(send, first, xs, False)
        all_lon(xs).wait_recv()
        for q in range(4):
            swapped = jnp.zeros((8, 128), F32)
            for n in range(8):
                row = jnp.broadcast_to(first[8 * q + n], (8, 128))
                row = pltpu.roll(row, 0, 1, stride=16, stride_axis=0)
                if n > 0:
                    row = pltpu.roll(row, 128 - 16 * n, 1)
                swapped = jnp.where(lanes8 == 7 - n, row, swapped)
            for i in range(NLAT):
                block[i, q : q + 1, :] = swapped[i : i + 1, :]
        block_to_lat(block, second, ys, False)
        all_lat(ys, 4).wait_recv()
        for i in range(NLAT):
            for q in range(4):
                row = jnp.broadcast_to(second[i, q : q + 1, :], (8, 128))
                row = pltpu.roll(row, 16, 1, stride=16, stride_axis=0)
                at = (i * 4 + q) * 8
                arrived[at : at + 8, :] = row
        return arrived[...]

    received = exchange(send1, first1, block1, second1, x1, y1)

    lane = iota((OBS, 128), 1)
    inst_lane = (lane & 15).astype(F32)
    err_row = err_wide[...]
    rinv_row = 1.0 / (err_row * err_row)
    row_w = iota((128, 128), 0)
    col_w = iota((128, 128), 1)
    ids = received.astype(BF16)
    for s in range(2):
        at = 8 * s
        here = slice(s * OBS, (s + 1) * OBS)
        l0 = iota((128, OBS), 0)
        pick = jnp.where(l0 == at, 1.0, 0.0) + jnp.where(l0 == at + 1, 48.0, 0.0)
        l1 = iota((OBS, 128), 1)
        pick_t = jnp.where(l1 == at, 1.0, 0.0) + jnp.where(l1 == at + 1, 48.0, 0.0)
        hot = dot(ids, pick.astype(BF16)) == square1.astype(F32)
        onehot[here, :] = hot.astype(F32).astype(BF16)
        hot_t = dot_t(pick_t.astype(BF16), ids) == square0.astype(F32)
        onehot_t[:, here] = hot_t.astype(F32).astype(BF16)
        instr = dot(ids, jnp.where(row_w == at + 2, 1.0, 0.0).astype(BF16))
        corner = jnp.where((row_w == at + 3 + (col_w >> 4)) & (col_w < 64), 1.0, 0.0)
        hit = instr == inst_lane
        chosen = dot(received, corner, lax.Precision.HIGHEST)
        spread_w[here, :] = jnp.where(hit, chosen, 0.0)
        err_hit = jnp.where(hit & (lane < 16), rinv_row, 0.0)
        inv = jnp.sum(err_hit, axis=1, keepdims=True)
        rinv[here, :] = jnp.broadcast_to(inv, (OBS, 128))
        obs_z[here, :] = jnp.broadcast_to(received[:, at + 7 : at + 8], (OBS, 128))

    ens_copy.wait()

    def gradient(weights):
        table = pick_rows(onehot_t[...], spread_w[...] * (rinv[...] * weights[...]))
        table = table[:CELLS]
        for h in range(2):
            wide = slice(h * 2 * LEV, (h + 1) * 2 * LEV)
            both = dot3(table, place_w[0, :, wide], place_w[1, :, wide])
            for c2 in range(2):
                field = both[:, c2 * LEV : (c2 + 1) * LEV]
                for t in range(WIN):
                    for pr in range(2):
                        at = (t * 2 + pr) * 24
                        grad[t, 2 * pr + h, pl.ds(c2, 24, stride=2), :] = field[
                            at : at + 24
                        ]

    def halo_copies(a, k):
        own = reg.at[a, k, pl.ds(ROWS, ROWS), OWN]
        north_rows = reg.at[a, k, pl.ds(0, ROWS), OWN]
        south_rows = reg.at[a, k, pl.ds(2 * ROWS, ROWS), OWN]
        w_strip = strip_send.at[a, k, 0]
        e_strip = strip_send.at[a, k, 1]

        def one(src, dst, part, i, j):
            return remote(src, dst, hs.at[a, part], hr.at[a, part, k], i, j)

        def corner(n, m):
            return corner_send.at[a, k, n], corner_recv.at[a, k, m]

        always = [
            one(w_strip, strip_recv.at[a, k, 1], 0, lat, west),
            one(e_strip, strip_recv.at[a, k, 0], 0, lat, east),
        ]
        to_n = [
            one(own, south_rows, 2, lat - 1, lon),
            one(*corner(0, 3), 2, lat - 1, west),
            one(*corner(1, 2), 2, lat - 1, east),
        ]
        to_s = [
            one(own, north_rows, 1, lat + 1, lon),
            one(*corner(2, 1), 1, lat + 1, west),
            one(*corner(3, 0), 1, lat + 1, east),
        ]
        return always, to_n, to_s

    def start_halo(a, k):
        always, to_n, to_s = halo_copies(a, k)

        @pl.when(has_n)
        def _():
            for c in to_n:
                c.start()

        @pl.when(has_s)
        def _():
            for c in to_s:
                c.start()

        for c in always:
            c.start()

    def wait_halo(a, k):
        rows_done(32, hs.at[a, 0], hr.at[a, 0, k]).wait_recv()

        @pl.when(has_n)
        def _():
            rows_done(CELLS + 16, hs.at[a, 1], hr.at[a, 1, k]).wait_recv()

        @pl.when(has_s)
        def _():
            rows_done(CELLS + 16, hs.at[a, 2], hr.at[a, 2, k]).wait_recv()

    def sent_halo(a):
        rows_done(FIELDS * 32, hs.at[a, 0], hr.at[a, 0, 0]).wait_send()

        @pl.when(has_s)
        def _():
            rows_done(FIELDS * (CELLS + 16), hs.at[a, 1], hr.at[a, 1, 0]).wait_send()

        @pl.when(has_n)
        def _():
            rows_done(FIELDS * (CELLS + 16), hs.at[a, 2], hr.at[a, 2, 0]).wait_send()

    def put_own(a, k, flat):
        for r in range(ROWS):
            row = flat[r * COLS : (r + 1) * COLS]
            reg[a, k, ROWS + r, PAD : PAD + COLS, :] = row
            strip_send[a, k, 0, 4 * r : 4 * r + 4, :] = row[0:4]
            strip_send[a, k, 1, 4 * r : 4 * r + 4, :] = row[COLS - 4 : COLS]
            for south in range(2):
                near = ROWS - 1 - r if south else r
                if near < 3:
                    at = (0, 3, 5)[near]
                    n = 3 - near
                    corner_send[a, k, 2 * south, at : at + n, :] = row[0:n]
                    corner_send[a, k, 2 * south + 1, at : at + n, :] = row[COLS - n : COLS]

    def send_fields(a):
        def member(k, c):
            summed = ens[k, 0].astype(F32) * grad[0]
            for t in range(1, WIN):
                summed = summed + ens[k, t].astype(F32) * grad[t]
            flat = dot3(summed.reshape(CELLS, LEV), level_w[0, 2], level_w[0, 3])
            put_own(a, k, BETA_ENSEMBLE * flat)
            start_halo(a, k)
            return c

        lax.fori_loop(0, MEM, member, 0)
        summed = (grad[0] + grad[1]) + (grad[2] + grad[3])
        flat = dot3(summed.reshape(CELLS, LEV), level_w[1, 2], level_w[1, 3])
        put_own(a, MEM, BETA_STATIC * flat)
        start_halo(a, MEM)

    def smooth(up, mid, down):
        side = pltpu.roll(mid, 1, 0) + pltpu.roll(mid, WIDE - 1, 0)
        return (1.0 - 4.0 * SMOOTH) * mid + SMOOTH * (up + down + side)

    def keep(row, value):
        if row < ROWS:
            return jnp.where(has_n, value, 0.0)
        if row >= 2 * ROWS:
            return jnp.where(has_s, value, 0.0)
        return value

    def spread_twice(a, k, note):
        for side, col in ((0, PAD - 4), (1, PAD + COLS)):
            for r in range(ROWS):
                reg[a, k, ROWS + r, col : col + 4, :] = strip_recv[
                    a, k, side, 4 * r : 4 * r + 4, :
                ]
            for south in range(2):
                for near in range(3):
                    at = (0, 3, 5)[near]
                    n = 3 - near
                    row = 2 * ROWS + near if south else ROWS - 1 - near
                    first_col = PAD + COLS if side else PAD - n
                    reg[a, k, row, first_col : first_col + n, :] = corner_recv[
                        a, k, 2 * south + side, at : at + n, :
                    ]

        def sweep(read, write, low, high):
            rows = [read(low - 1), read(low)]
            for r in range(low, high):
                rows.append(read(r + 1))
                write(r, keep(r, smooth(rows[0], rows[1], rows[2])))
                rows = rows[1:]

        def to_a(r, v):
            stage_a[r] = v

        def to_b(r, v):
            stage_b[r] = v

        sweep(lambda r: keep(r, reg[a, k, r]), to_a, 1, TALL - 1)
        sweep(lambda r: stage_a[r], to_b, 2, TALL - 2)
        for r in range(ROWS):
            note(k, r, stage_b[ROWS + r, PAD : PAD + COLS, :])
        sweep(lambda r: stage_b[r], to_a, 3, TALL - 3)
        sweep(lambda r: stage_a[r], to_b, 4, TALL - 4)
        rows = [stage_b[ROWS + r, PAD : PAD + COLS, :] for r in range(ROWS)]
        return jnp.concatenate(rows, axis=0)

    def apply_fields(a, target, note):
        def member(k, c):
            wait_halo(a, k)
            local = dot3(spread_twice(a, k, note), level_w[0, 0], level_w[0, 1])
            local = (BETA_ENSEMBLE * local).reshape(ROWS, COLS, LEV)
            for t in range(WIN):
                incr[t] += ens[k, t].astype(F32) * local
            return c

        lax.fori_loop(0, MEM, member, 0)
        wait_halo(a, MEM)
        part = dot3(spread_twice(a, MEM, note), level_w[1, 0], level_w[1, 1])
        part = (BETA_STATIC * part).reshape(ROWS, COLS, LEV)
        for t in range(WIN):
            incr[t] += part
        seen = jnp.zeros((CELLS, 128), F32)
        for h in range(2):
            pair = []
            for c2 in range(2):
                cells = [
                    incr[t, 2 * pr + h, pl.ds(c2, 24, stride=2), :]
                    for t in range(WIN)
                    for pr in range(2)
                ]
                pair.append(jnp.concatenate(cells, axis=0))
            tall = slice(h * 2 * LEV, (h + 1) * 2 * LEV)
            seen = seen + dot3(
                jnp.concatenate(pair, axis=1), place_wt[0, tall, :], place_wt[1, tall, :]
            )
        seen = jnp.concatenate([seen, jnp.zeros((OBS - CELLS, 128), F32)], axis=0)
        value = pick_rows(onehot[...], seen) * spread_w[...]
        value = jnp.sum(value, axis=1, keepdims=True)
        target[...] = jnp.broadcast_to(value, (SLOTS, 128))

    def note_first(k, r, v):
        resid[0, k, r] = v
        acc[0] += fold(v * v)

    gradient(obs_z)
    send_fields(0)
    apply_fields(0, obs_e, note_first)
    out0 = pltpu.make_async_copy(resid.at[0], out_fields.at[0], out_sem.at[0])
    out0.start()
    sum_a = total(acc[0])
    first_e = obs_e[...]
    sum_b = jnp.sum(rinv[...] * first_e * first_e, axis=0, keepdims=True)[:, 0:1]
    lane1 = iota((1, 128), 1)
    red_a_send[...] = jnp.where(lane1 == 0, sum_a, 0.0) + jnp.where(lane1 == 1, sum_b, 0.0)
    block_to_lat(red_a_send, red_a, ra, True)

    incr[...] = jnp.zeros_like(incr)
    acc[...] = jnp.zeros_like(acc)
    gradient(obs_e)
    send_fields(1)
    all_lat(ra, 1).wait_recv()
    part = red_a[0]
    for i in range(1, NLAT):
        part = part + red_a[i]
    red_b_send[...] = part
    rows_to_lon(red_b_send, red_b, rb, True)
    all_lon(rb).wait_recv()
    whole = red_b[0]
    for j in range(1, NLON):
        whole = whole + red_b[j]
    a0 = whole[:, 0:1]
    b0 = whole[:, 1:2]
    step0 = a0 / (a0 + b0)
    rest0 = b0 / (a0 + b0)

    def note_second(k, r, v):
        r0 = resid[0, k, r]
        r1 = rest0 * r0 - step0 * v
        resid[1, k, r] = r1
        acc[0] += fold(r1 * r1)
        acc[1] += fold(r1 * r0)

    apply_fields(1, obs_z, note_second)
    out1 = pltpu.make_async_copy(resid.at[1], out_fields.at[1], out_sem.at[1])
    out1.start()

    partial = [total(acc[0]), total(acc[1])]
    sum_v = jnp.zeros((1, 1), F32)
    sum_w = jnp.zeros((1, 1), F32)
    blocks = jnp.zeros((OBS, 128), F32)
    word = lane & 15
    for s in range(2):
        here = slice(s * OBS, (s + 1) * OBS)
        e = obs_e[here, :]
        nxt = rest0 * e - step0 * obs_z[here, :]
        weighted = rinv[here, :] * nxt
        sum_v = sum_v + jnp.sum(weighted * nxt, axis=0, keepdims=True)[:, 0:1]
        sum_w = sum_w + jnp.sum(weighted * e, axis=0, keepdims=True)[:, 0:1]
        blocks = jnp.where(word == s, e, blocks)
        blocks = jnp.where(word == 2 + s, nxt, blocks)
    partial = partial + [sum_v, sum_w]
    for n in range(4):
        blocks = jnp.where(word == 4 + n, partial[n], blocks)
    blocks = jnp.where((lane >> 4) == 7 - (iota((OBS, 128), 0) >> 5), blocks, 0.0)
    out_rows = blocks[0:NLON]
    for i in range(1, NLAT):
        out_rows = out_rows + blocks[i * NLON : (i + 1) * NLON]
    for j in range(NLON):
        send2[j] = out_rows[j : j + 1, :]

    back = exchange(send2, first2, block2, second2, x2, y2)
    sums = jnp.sum(back, axis=0, keepdims=True)
    rr1, u, v, w = [sums[:, 4 + n : 5 + n] for n in range(4)]
    ratio = rr1 / a0
    below = (rr1 + 2.0 * ratio * u + ratio * ratio * a0) + (
        v + 2.0 * ratio * w + ratio * ratio * b0
    )
    step1 = rr1 / below
    c0 = step0 + step1 * ratio
    c1 = step1
    out_coef[...] = jnp.where(iota((2, 128), 0) == 0, c0, c1)

    mine = dest_row == square0
    equiv = jnp.zeros((1, OBS), F32)
    for s in range(2):
        value = c0 * back[:, s : s + 1] + c1 * back[:, 2 + s : 3 + s]
        chosen = jnp.where(mine & (rank == float(s)), value, 0.0)
        equiv = equiv + jnp.sum(chosen, axis=0, keepdims=True)
    out_equiv[...] = equiv

    out0.wait()
    out1.wait()
    for sems in (x1, x2, rb):
        all_lon(sems).wait_send()
    for sems, rows in ((y1, 4), (y2, 4), (ra, 1)):
        all_lat(sems, rows).wait_send()
    sent_halo(0)
    sent_halo(1)


def finish(fields, coef, equiv, out_static, out_member, out_equiv, held, made, sem_in, sem_out):
    loads = [
        [pltpu.make_async_copy(fields.at[a, k], held.at[a, k], sem_in.at[a, k]) for a in range(2)]
        for k in range(FIELDS)
    ]
    for pair in loads:
        for c in pair:
            c.start()
    out_equiv[...] = equiv[...]
    c0 = coef[0:1, :]
    c1 = coef[1:2, :]
    stores = []
    for k in range(FIELDS):
        for c in loads[k]:
            c.wait()
        for r in range(ROWS):
            made[k, r] = c0 * held[0, k, r] + c1 * held[1, k, r]
        target = out_static if k == MEM else out_member.at[k]
        stores.append(pltpu.make_async_copy(made.at[k], target, sem_out.at[k]))
        stores[-1].start()
    for c in stores:
        c.wait()


def body(
    ensemble, vert_loc, static_vert, inst_vert, inst_err, obs_dest, obs_patch,
    obs_window, obs_inst, obs_hweight, innovation, obs_count,
):
    vmem = pl.BlockSpec(memory_space=pltpu.VMEM)
    anywhere = pl.BlockSpec(memory_space=pl.ANY)
    hbm = pl.BlockSpec(memory_space=pltpu.HBM)
    dma = pltpu.SemaphoreType.DMA
    ints = jnp.int32
    exchange = [
        pltpu.VMEM((NLON, 1, 128), F32),
        pltpu.VMEM((NLON, 1, 128), F32),
        pltpu.VMEM((NLAT, 4, 128), F32),
        pltpu.VMEM((NLAT, 4, 128), F32),
    ]
    scratch = [
        pltpu.VMEM((MEM, WIN, ROWS, COLS, LEV), BF16),
        pltpu.VMEM((LEV, LEV), F32),
        pltpu.VMEM((LEV, LEV), F32),
        pltpu.VMEM((NINST, LEV), F32),
        pltpu.VMEM((1, NINST), F32),
        pltpu.VMEM((1, OBS), ints),
        pltpu.VMEM((1, OBS), ints),
        pltpu.VMEM((1, OBS), ints),
        pltpu.VMEM((1, OBS), ints),
        pltpu.VMEM((4, OBS), F32),
        pltpu.VMEM((1, OBS), F32),
        pltpu.VMEM((1, 128), F32),
        *exchange,
        *exchange,
        pltpu.VMEM((OBS, 128), F32),
        pltpu.VMEM((1, 128), F32),
        pltpu.VMEM((NLAT, 1, 128), F32),
        pltpu.VMEM((1, 128), F32),
        pltpu.VMEM((NLON, 1, 128), F32),
        pltpu.VMEM((2, 4, LEV, LEV), BF16),
        pltpu.VMEM((128, 4 * LEV), F32),
        pltpu.VMEM((2, 128, 4 * LEV), BF16),
        pltpu.VMEM((2, 4 * LEV, 128), BF16),
        pltpu.VMEM((SLOTS, OBS), BF16),
        pltpu.VMEM((OBS, SLOTS), BF16),
        pltpu.VMEM((SLOTS, 128), F32),
        pltpu.VMEM((SLOTS, 128), F32),
        pltpu.VMEM((SLOTS, 128), F32),
        pltpu.VMEM((SLOTS, 128), F32),
        pltpu.VMEM((WIN, ROWS, COLS, LEV), F32),
        pltpu.VMEM((WIN, ROWS, COLS, LEV), F32),
        pltpu.VMEM((2, FIELDS, TALL, WIDE, LEV), F32),
        pltpu.VMEM((2, FIELDS, 2, 16, LEV), F32),
        pltpu.VMEM((2, FIELDS, 2, 16, LEV), F32),
        pltpu.VMEM((2, FIELDS, 4, 8, LEV), F32),
        pltpu.VMEM((2, FIELDS, 4, 8, LEV), F32),
        pltpu.VMEM((FIELDS * (CELLS + 16), 128), F32),
        pltpu.VMEM((TALL, WIDE, LEV), F32),
        pltpu.VMEM((TALL, WIDE, LEV), F32),
        pltpu.VMEM((2, FIELDS, ROWS, COLS, LEV), F32),
        pltpu.VMEM((2, 8, LEV), F32),
        dma((10,)), dma(()), dma((2,)),
        dma((2,)), dma((2,)), dma((2,)), dma((2,)), dma((2,)), dma((2,)),
        dma((2, 3)), dma((2, 3, FIELDS)),
    ]
    fields, coef, equiv = pl.pallas_call(
        kernel,
        out_shape=(
            jax.ShapeDtypeStruct((2, FIELDS, ROWS, COLS, LEV), F32),
            jax.ShapeDtypeStruct((2, 128), F32),
            jax.ShapeDtypeStruct((1, OBS), F32),
        ),
        in_specs=[pl.BlockSpec(memory_space=pltpu.SMEM)] + [hbm] * 11,
        out_specs=(anywhere, vmem, vmem),
        scratch_shapes=scratch,
        compiler_params=pltpu.CompilerParams(
            collective_id=0, has_side_effects=True, vmem_limit_bytes=67043328
        ),
        name="inner_loop",
    )(
        obs_count, ensemble, vert_loc, static_vert, inst_vert,
        inst_err.reshape(1, NINST), obs_dest.reshape(1, OBS),
        obs_patch.reshape(1, OBS), obs_window.reshape(1, OBS),
        obs_inst.reshape(1, OBS), obs_hweight, innovation.reshape(1, OBS),
    )
    static, member, equiv = pl.pallas_call(
        finish,
        out_shape=(
            jax.ShapeDtypeStruct((ROWS, COLS, LEV), F32),
            jax.ShapeDtypeStruct((MEM, ROWS, COLS, LEV), F32),
            jax.ShapeDtypeStruct((1, OBS), F32),
        ),
        in_specs=[hbm, vmem, vmem],
        out_specs=(hbm, hbm, vmem),
        scratch_shapes=[
            pltpu.VMEM((2, FIELDS, ROWS, COLS, LEV), F32),
            pltpu.VMEM((FIELDS, ROWS, COLS, LEV), F32),
            dma((2, FIELDS)),
            dma((FIELDS,)),
        ],
        compiler_params=pltpu.CompilerParams(vmem_limit_bytes=67043328),
        name="finish",
    )(fields, coef, equiv)
    return static, member, equiv.reshape(OBS)


def solution(mesh):
    both = ("lat", "lon")
    in_specs = (
        P(None, None, "lat", "lon", None), P(), P(), P(), P(), P(both, None),
        P(both), P(both), P(both), P(None, both), P(both), P(both),
    )
    out_specs = (P("lat", "lon", None), P(None, "lat", "lon", None), P(both))
    return jax.shard_map(
        body, mesh=mesh, in_specs=in_specs, out_specs=out_specs, check_vma=False
    )
```

time: 96.2 us -> 68.3 us (0.71)
  Pallas kernels: 87.8 us -> 66.8 us
  local copies, waits for them, and re-layouts: 6.9 us -> 0 us
    pallas_call x1 -> x2, Pallas kernels: 87.8 us -> 66.8 us  [the longest x1 63.1 us: body(): pl.pallas_call(kernel, out_shape=(jax.ShapeDtypeStruct((2, FIELDS, ROWS,...]
    unnamed x6 -> x0, local copies, waits for them, and re-layouts: 5.65 us -> none
    another operation x2 -> x0, local copies, waits for them, and re-layouts: 1.25 us -> none  [body(): jnp.tile(inst_err, 8).reshape(1, 128)]
where the time goes in v1:
time: 68.3 us; the launch traced here: 68.1 us
  Pallas kernels  66.8 us (98%)
  between operations  1.29 us (2%)
    pallas_call x1, Pallas kernels, body(): pl.pallas_call(kernel, out_shape=(jax.ShapeDtypeStruct((2, FIELDS, ROWS,...  63.1 us
    pallas_call x1, Pallas kernels, body(): pl.pallas_call(finish, out_shape=(jax.ShapeDtypeStruct((ROWS, COLS, LEV),...  3.65 us

profile of v1, /device:TPU:1, one launch (start us, length us, event | category | flops | bytes accessed | tf_op | source)
XLA Modules:
  0.0 68.1 jit_solution(13860422090750658249)
XLA Ops:
  1.3 63.1 %inner_loop.1 = (f32[2,9,4,48,128]{4,3,2,1,0:T(8,128)}, f32[2,128]{1,0:T(2,128)}, f32[1,256]{1,0:T(1,128)}) custom-call(s32[1]{0:T(128)S(6)} %copy.15.count_ref, bf16[8,4,4,48,128]{4,3,2,1,0:T(8,128)(2,1)} %ens_hbm.1, f32[128,128]{1,0:T(8,128)} %vert_hbm.1, f32[128,128]{1,0:T(8,128)} %static_hbm.1, f32[16,128]{1,0:T(8,128)} %inst_hbm.1, f32[1,16]{1,0:T(1,128)} %bitcast.12, ...), custom_call_target="tpu_custom_call" | custom-call | tf_op jit(solution)/shard_map/inner_loop/pallas_call | solution.py:639
  64.4 3.6 %finish.1 = (f32[4,48,128]{2,1,0:T(8,128)}, f32[8,4,48,128]{3,2,1,0:T(8,128)}, f32[1,256]{1,0:T(1,128)}) custom-call(f32[2,9,4,48,128]{4,3,2,1,0:T(8,128)} %get-tuple-element.9.fields, f32[2,128]{1,0:T(2,128)} %get-tuple-element.10.coef, f32[1,256]{1,0:T(1,128)} %get-tuple-element.11.equiv), custom_call_target="tpu_custom_call" | custom-call | tf_op jit(solution)/shard_map/finish/pallas_call | solution.py:659

commit v2 on v1

--- a/solution.py
+++ b/solution.py
@@ -14,6 +14,7 @@
 NLAT, NLON = 8, 32
 MEM, WIN, ROWS, COLS, LEV, NINST = 8, 4, 4, 48, 128, 16
 FIELDS = MEM + 1
+EARLY = 6
 CELLS = ROWS * COLS
 OBS = 256
 SLOTS = 2 * OBS
@@ -81,17 +82,26 @@
     west = lax.rem(lon + NLON - 1, NLON)
     east = lax.rem(lon + 1, NLON)
 
+    big = lat * 4 + lon // 8
+    little = lax.rem(lon, 8)
+
+    def big_peer(j):
+        return j // 4, lax.rem(j, 4) * 8 + little
+
+    def little_peer(i):
+        return lat, (lon // 8) * 8 + i
+
     barrier = pltpu.get_barrier_semaphore()
 
     def greet(i, j):
         pl.semaphore_signal(barrier, inc=1, device_id=(i, j), device_id_type=MESH)
 
-    def greet_lon(d, c):
-        greet(lat, lax.rem(lon + d, NLON))
+    def greet_big(d, c):
+        greet(*big_peer(lax.rem(big + d, NLON)))
         return c
 
-    def greet_lat(d, c):
-        greet(lax.rem(lat + d, NLAT), lon)
+    def greet_little(d, c):
+        greet(*little_peer(lax.rem(little + d, NLAT)))
         return c
 
     small = [
@@ -105,9 +115,9 @@
     ]
     for c in loads:
         c.start()
-    lax.fori_loop(1, NLON, greet_lon, 0)
-    lax.fori_loop(1, NLAT, greet_lat, 0)
-    for step in (1, NLAT - 1):
+    lax.fori_loop(1, NLON, greet_big, 0)
+    lax.fori_loop(1, NLAT, greet_little, 0)
+    for step in (0, 1, NLAT - 1):
         greet(lax.rem(lat + step, NLAT), west)
         greet(lax.rem(lat + step, NLAT), east)
     ens_copy = pltpu.make_async_copy(ens_hbm, ens, ens_sem)
@@ -116,6 +126,7 @@
         c.wait()
 
     dest_row = dest_ref[...]
+    dest_row = (dest_row & 7) * 32 + (dest_row >> 3)
     square0 = iota((OBS, OBS), 0)
     square1 = iota((OBS, OBS), 1)
     dest_f = jnp.where(square0 == square1, dest_row.astype(F32), 0.0)
@@ -136,8 +147,8 @@
     )
     tiled = jnp.concatenate([words] * 16, axis=0)
     tiled = jnp.where((iota((128, OBS), 0) >> 3) == group, tiled, 0.0)
-    to_lon = (iota((NLON, OBS), 0) == (dest_row & 31)).astype(F32)
-    outgoing = dot_t(to_lon, tiled, lax.Precision.HIGHEST)
+    to_big = (iota((NLON, OBS), 0) == (dest_row & 31)).astype(F32)
+    outgoing = dot_t(to_big, tiled, lax.Precision.HIGHEST)
     for j in range(NLON):
         send1[j] = outgoing[j : j + 1, :]
 
@@ -161,7 +172,7 @@
     acc[...] = jnp.zeros_like(acc)
     incr[...] = jnp.zeros_like(incr)
 
-    pl.semaphore_wait(barrier, NLON - 1 + NLAT - 1 + 4)
+    pl.semaphore_wait(barrier, NLON - 1 + NLAT - 1 + 6)
 
     def remote(src, dst, ssem, rsem, i, j):
         return pltpu.make_async_remote_copy(
@@ -173,37 +184,38 @@
         ref = tally.at[pl.ds(0, rows)]
         return remote(ref, ref, ssem, rsem, lat, east)
 
-    def rows_to_lon(send, first, sems, one_row):
+    def rows_to_big(send, first, sems, one_row):
         def go(d, c):
-            j = lax.rem(lon + d, NLON)
+            j = lax.rem(big + d, NLON)
             src = send if one_row else send.at[j]
-            remote(src, first.at[lon], sems.at[0], sems.at[1], lat, j).start()
+            remote(src, first.at[big], sems.at[0], sems.at[1], *big_peer(j)).start()
             return c
 
         lax.fori_loop(1, NLON, go, 0)
-        first[lon] = send[...] if one_row else send[lon]
-
-    def all_lon(sems):
+        first[big] = send[...] if one_row else send[big]
+
+    def all_big(sems):
         return rows_done(NLON - 1, sems.at[0], sems.at[1])
 
-    def block_to_lat(send, second, sems, whole):
+    def block_to_little(send, second, sems, whole):
         def go(d, c):
-            i = lax.rem(lat + d, NLAT)
+            i = lax.rem(little + d, NLAT)
             src = send if whole else send.at[i]
-            remote(src, second.at[lat], sems.at[0], sems.at[1], i, lon).start()
+            to = little_peer(i)
+            remote(src, second.at[little], sems.at[0], sems.at[1], *to).start()
             return c
 
         lax.fori_loop(1, NLAT, go, 0)
-        second[lat] = send[...] if whole else send[lat]
-
-    def all_lat(sems, rows):
+        second[little] = send[...] if whole else send[little]
+
+    def all_little(sems, rows):
         return rows_done((NLAT - 1) * rows, sems.at[0], sems.at[1])
 
     lanes8 = iota((8, 128), 1) >> 4
 
     def exchange(send, first, block, second, xs, ys):
-        rows_to_lon(send, first, xs, False)
-        all_lon(xs).wait_recv()
+        rows_to_big(send, first, xs, False)
+        all_big(xs).wait_recv()
         for q in range(4):
             swapped = jnp.zeros((8, 128), F32)
             for n in range(8):
@@ -214,8 +226,8 @@
                 swapped = jnp.where(lanes8 == 7 - n, row, swapped)
             for i in range(NLAT):
                 block[i, q : q + 1, :] = swapped[i : i + 1, :]
-        block_to_lat(block, second, ys, False)
-        all_lat(ys, 4).wait_recv()
+        block_to_little(block, second, ys, False)
+        all_little(ys, 4).wait_recv()
         for i in range(NLAT):
             for q in range(4):
                 row = jnp.broadcast_to(second[i, q : q + 1, :], (8, 128))
@@ -417,7 +429,7 @@
         rows = [stage_b[ROWS + r, PAD : PAD + COLS, :] for r in range(ROWS)]
         return jnp.concatenate(rows, axis=0)
 
-    def apply_fields(a, target, note):
+    def apply_members(a, start, stop, note):
         def member(k, c):
             wait_halo(a, k)
             local = dot3(spread_twice(a, k, note), level_w[0, 0], level_w[0, 1])
@@ -426,7 +438,9 @@
                 incr[t] += ens[k, t].astype(F32) * local
             return c
 
-        lax.fori_loop(0, MEM, member, 0)
+        lax.fori_loop(start, stop, member, 0)
+
+    def apply_static(a, target, note):
         wait_halo(a, MEM)
         part = dot3(spread_twice(a, MEM, note), level_w[1, 0], level_w[1, 1])
         part = (BETA_STATIC * part).reshape(ROWS, COLS, LEV)
@@ -457,7 +471,8 @@
 
     gradient(obs_z)
     send_fields(0)
-    apply_fields(0, obs_e, note_first)
+    apply_members(0, 0, MEM, note_first)
+    apply_static(0, obs_e, note_first)
     out0 = pltpu.make_async_copy(resid.at[0], out_fields.at[0], out_sem.at[0])
     out0.start()
     sum_a = total(acc[0])
@@ -465,22 +480,27 @@
     sum_b = jnp.sum(rinv[...] * first_e * first_e, axis=0, keepdims=True)[:, 0:1]
     lane1 = iota((1, 128), 1)
     red_a_send[...] = jnp.where(lane1 == 0, sum_a, 0.0) + jnp.where(lane1 == 1, sum_b, 0.0)
-    block_to_lat(red_a_send, red_a, ra, True)
+    rows_to_big(red_a_send, red_a, ra, True)
 
     incr[...] = jnp.zeros_like(incr)
     acc[...] = jnp.zeros_like(acc)
     gradient(obs_e)
     send_fields(1)
-    all_lat(ra, 1).wait_recv()
+    def note_early(k, r, v):
+        resid[1, k, r] = v
+
+    apply_members(1, 0, 1, note_early)
+    all_big(ra).wait_recv()
     part = red_a[0]
+    for j in range(1, NLON):
+        part = part + red_a[j]
+    red_b_send[...] = part
+    block_to_little(red_b_send, red_b, rb, True)
+    apply_members(1, 1, EARLY, note_early)
+    all_little(rb, 1).wait_recv()
+    whole = red_b[0]
     for i in range(1, NLAT):
-        part = part + red_a[i]
-    red_b_send[...] = part
-    rows_to_lon(red_b_send, red_b, rb, True)
-    all_lon(rb).wait_recv()
-    whole = red_b[0]
-    for j in range(1, NLON):
-        whole = whole + red_b[j]
+        whole = whole + red_b[i]
     a0 = whole[:, 0:1]
     b0 = whole[:, 1:2]
     step0 = a0 / (a0 + b0)
@@ -493,7 +513,14 @@
         acc[0] += fold(r1 * r1)
         acc[1] += fold(r1 * r0)
 
-    apply_fields(1, obs_z, note_second)
+    def catch_up(k, c):
+        for r in range(ROWS):
+            note_second(k, r, resid[1, k, r])
+        return c
+
+    lax.fori_loop(0, EARLY, catch_up, 0)
+    apply_members(1, EARLY, MEM, note_second)
+    apply_static(1, obs_z, note_second)
     out1 = pltpu.make_async_copy(resid.at[1], out_fields.at[1], out_sem.at[1])
     out1.start()
 
@@ -543,10 +570,10 @@
 
     out0.wait()
     out1.wait()
-    for sems in (x1, x2, rb):
-        all_lon(sems).wait_send()
-    for sems, rows in ((y1, 4), (y2, 4), (ra, 1)):
-        all_lat(sems, rows).wait_send()
+    for sems in (x1, x2, ra):
+        all_big(sems).wait_send()
+    for sems, rows in ((y1, 4), (y2, 4), (rb, 1)):
+        all_little(sems, rows).wait_send()
     sent_halo(0)
     sent_halo(1)
 
@@ -607,9 +634,9 @@
         *exchange,
         pltpu.VMEM((OBS, 128), F32),
         pltpu.VMEM((1, 128), F32),
+        pltpu.VMEM((NLON, 1, 128), F32),
+        pltpu.VMEM((1, 128), F32),
         pltpu.VMEM((NLAT, 1, 128), F32),
-        pltpu.VMEM((1, 128), F32),
-        pltpu.VMEM((NLON, 1, 128), F32),
         pltpu.VMEM((2, 4, LEV, LEV), BF16),
         pltpu.VMEM((128, 4 * LEV), F32),
         pltpu.VMEM((2, 128, 4 * LEV), BF16),

time: 68.3 us -> 67.7 us (level)
  no operation moved by 1% of the time
where the time goes in v2:
time: 67.7 us; the launch traced here: 67.5 us
  Pallas kernels  66.2 us (98%)
  between operations  1.29 us (2%)
    pallas_call x1, Pallas kernels, body(): pl.pallas_call(kernel, out_shape=(jax.ShapeDtypeStruct((2, FIELDS, ROWS,...  62.6 us
    pallas_call x1, Pallas kernels, body(): pl.pallas_call(finish, out_shape=(jax.ShapeDtypeStruct((ROWS, COLS, LEV),...  3.65 us

profile of v2, /device:TPU:1, one launch (start us, length us, event | category | flops | bytes accessed | tf_op | source)
XLA Modules:
  0.0 67.5 jit_solution(5651207970133967719)
XLA Ops:
  1.3 62.6 %inner_loop.1 = (f32[2,9,4,48,128]{4,3,2,1,0:T(8,128)}, f32[2,128]{1,0:T(2,128)}, f32[1,256]{1,0:T(1,128)}) custom-call(s32[1]{0:T(128)S(6)} %copy.15.count_ref, bf16[8,4,4,48,128]{4,3,2,1,0:T(8,128)(2,1)} %ens_hbm.1, f32[128,128]{1,0:T(8,128)} %vert_hbm.1, f32[128,128]{1,0:T(8,128)} %static_hbm.1, f32[16,128]{1,0:T(8,128)} %inst_hbm.1, f32[1,16]{1,0:T(1,128)} %bitcast.12, ...), custom_call_target="tpu_custom_call" | custom-call | tf_op jit(solution)/shard_map/inner_loop/pallas_call | solution.py:666
  63.8 3.6 %finish.1 = (f32[4,48,128]{2,1,0:T(8,128)}, f32[8,4,48,128]{3,2,1,0:T(8,128)}, f32[1,256]{1,0:T(1,128)}) custom-call(f32[2,9,4,48,128]{4,3,2,1,0:T(8,128)} %get-tuple-element.9.fields, f32[2,128]{1,0:T(2,128)} %get-tuple-element.10.coef, f32[1,256]{1,0:T(1,128)} %get-tuple-element.11.equiv), custom_call_target="tpu_custom_call" | custom-call | tf_op jit(solution)/shard_map/finish/pallas_call | solution.py:686
